TPU v7x, 32 devices: a whole 2x2x4 slice. The times are simulated.
32 devices in a mesh: seq: 16 (over z, x, core), head: 2 (over y).
Axes of the slice: x: 2, y: 2, z: 4, core: 2. Of those that a mesh axis runs over, the one named last changes fastest.
Arguments:
- prompt_token_query: bfloat16 [512, 8192], P('seq', 'head'), may hold values from -6 to 6
- prompt_token_key: bfloat16 [512, 1024], P('seq', 'head'), may hold values from -6 to 6
- prompt_token_value: bfloat16 [512, 1024], P('seq', 'head'), may hold values from -6 to 6
- response_query_slots: bfloat16 [3072, 8192], P('seq', 'head'), may hold values from -160 to 160
- response_key_slots: bfloat16 [3072, 1024], P('seq', 'head'), may hold values from -6 to 6
- response_value_slots: bfloat16 [3072, 1024], P('seq', 'head'), may hold values from -6 to 6
- lengths: int32 [4], replicated, may hold values from 1 to 8, 16 in all
- block_table: int32 [16], replicated, may hold values from 0 to 15, each once
Outputs:
- prompt_out: bfloat16 [512, 8192], P(('seq', 'head'))
- answer_out: bfloat16 [3072, 8192], P(('seq', 'head'))
Inputs may be any that keep to these rules, and one draw needn't show every extreme that they name: `lengths`: they sum to 16; the largest is exactly 8. `block_table`: A permutation of 0 to 15.
All inputs are finite; a program needn't handle non-finite values.
Results may differ from a plain program's by a relative error of at most 0.007.
Values may be sent and summed in bfloat16 or wider, within the bound.
A program may use at most 64 MiB of HBM per device.

v0:
```python
import math

import jax
import jax.numpy as jnp
from jax import lax
from jax.sharding import PartitionSpec as P

HEAD_SIZE = 128
RESPONSE_BLOCK = 192


NEG_FILL = -1e30


def block_roles(lengths, global_blocks):
    bounds = jnp.cumsum(lengths)
    member = jnp.sum((global_blocks[:, None] >= bounds[None, :]).astype(jnp.int32), axis=1)
    starts = bounds - lengths
    owner_match = member[:, None] == jnp.arange(lengths.shape[0], dtype=jnp.int32)[None, :]
    first_block = jnp.sum(jnp.where(owner_match, starts[None, :], 0), axis=1)
    return (member, global_blocks - first_block, first_block)


def empty_state(row_count, heads_kv, query_group_width):
    peak_value = jnp.full((row_count, heads_kv, query_group_width), NEG_FILL, jnp.float32)
    weight_total = jnp.zeros((row_count, heads_kv, query_group_width), jnp.float32)
    mixed_sum = jnp.zeros((row_count, heads_kv, query_group_width, HEAD_SIZE), jnp.float32)
    return (peak_value, weight_total, mixed_sum)


def score_block(query_matrix, key_rows):
    return jnp.einsum(
        "rjgd,sjd->rjgs", query_matrix, key_rows, preferred_element_type=jnp.float32
    ) * HEAD_SIZE ** (-0.5)


def absorb(softmax_state, scores, visible, value_rows):
    peak_old, total_old, mixed_old = softmax_state
    masked = jnp.where(visible, scores, NEG_FILL)
    peak_new = jnp.maximum(peak_old, jnp.max(masked, axis=-1))
    factor = jnp.exp(peak_old - peak_new)
    weights = jnp.where(visible, jnp.exp(scores - peak_new[..., None]), 0.0)
    total_new = total_old * factor + jnp.sum(weights, axis=-1)
    mixed_new = mixed_old * factor[..., None] + jnp.einsum(
        "rjgs,sjd->rjgd",
        weights.astype(jnp.bfloat16),
        value_rows,
        preferred_element_type=jnp.float32,
    )
    return (peak_new, total_new, mixed_new)


def finish(softmax_state):
    peak_value, weight_total, mixed_sum = softmax_state
    row_count = mixed_sum.shape[0]
    return (mixed_sum / weight_total[..., None]).astype(jnp.bfloat16).reshape(row_count, -1)


def on_device(
    prompt_token_query,
    prompt_token_key,
    prompt_token_value,
    response_query_slots,
    response_key_slots,
    response_value_slots,
    lengths,
    block_table,
):
    heads_kv = response_key_slots.shape[1] // HEAD_SIZE
    heads_query = response_query_slots.shape[1] // HEAD_SIZE
    query_group_width = heads_query // heads_kv
    shard_rows = response_query_slots.shape[0]
    slot_count = shard_rows // RESPONSE_BLOCK
    prompt_rows = prompt_token_query.shape[0]
    most_blocks = block_table.shape[0] // 2
    batch_blocks = 4
    seq_place = lax.axis_index("seq")
    own_blocks = lax.dynamic_slice_in_dim(block_table, seq_place * slot_count, slot_count, 0)
    own_member, own_position, unused_first = block_roles(lengths, own_blocks)
    answer_queries = response_query_slots.reshape(
        slot_count, RESPONSE_BLOCK, heads_kv, query_group_width, HEAD_SIZE
    )
    prompt_queries = prompt_token_query.reshape(prompt_rows, heads_kv, query_group_width, HEAD_SIZE)
    prompt_positions = seq_place * prompt_rows + jnp.arange(prompt_rows, dtype=jnp.int32)
    initial = (
        tuple(
            (
                empty_state(RESPONSE_BLOCK, heads_kv, query_group_width)
                for slot_ordinal in range(slot_count)
            )
        ),
        empty_state(prompt_rows, heads_kv, query_group_width),
    )
    carried = initial
    piece_key = lax.all_gather(prompt_token_key, "seq", axis=0, tiled=True)
    piece_value = lax.all_gather(prompt_token_value, "seq", axis=0, tiled=True)
    row_count = piece_key.shape[0]
    part_width = math.gcd(row_count, prompt_rows * max(1, 256 // prompt_rows))
    part_count = row_count // part_width
    key_parts = piece_key.reshape(part_count, part_width, heads_kv, HEAD_SIZE)
    value_parts = piece_value.reshape(part_count, part_width, heads_kv, HEAD_SIZE)
    offsets = jnp.arange(part_count, dtype=jnp.int32) * part_width

    def one_part(state_in, part_data):
        key_rows, value_rows, offset = part_data
        answer_states, prompt_state = state_in
        all_seen = jnp.ones((1, 1, 1, part_width), dtype=bool)
        answer_states = tuple(
            (
                absorb(
                    answer_states[slot_ordinal],
                    score_block(answer_queries[slot_ordinal], key_rows),
                    all_seen,
                    value_rows,
                )
                for slot_ordinal in range(slot_count)
            )
        )
        key_positions = offset + jnp.arange(part_width, dtype=jnp.int32)
        seen = (key_positions[None, :] <= prompt_positions[:, None])[:, None, None, :]
        prompt_state = absorb(prompt_state, score_block(prompt_queries, key_rows), seen, value_rows)
        return ((answer_states, prompt_state), None)

    carried, unused_out = lax.scan(one_part, carried, (key_parts, value_parts, offsets))
    finished = carried
    piece_key = lax.all_gather(response_key_slots, "seq", axis=0, tiled=True)
    piece_value = lax.all_gather(response_value_slots, "seq", axis=0, tiled=True)
    block_total = piece_key.shape[0] // RESPONSE_BLOCK
    batch_count = -(-min(most_blocks, block_total) // batch_blocks)
    picked_total = batch_count * batch_blocks
    blocked_keys = piece_key.reshape(block_total, RESPONSE_BLOCK, heads_kv, HEAD_SIZE)
    blocked_values = piece_value.reshape(block_total, RESPONSE_BLOCK, heads_kv, HEAD_SIZE)
    piece_member, piece_position, unused_start = block_roles(lengths, block_table)
    block_ids = jnp.arange(block_total, dtype=jnp.int32)
    answer_states, prompt_state = finished
    slot_ordinal = 0
    wanted = (piece_member == own_member[slot_ordinal]) & (
        piece_position <= own_position[slot_ordinal]
    )
    ranking = jnp.cumsum(wanted.astype(jnp.int32)) - 1
    matches = wanted[None, :] & (
        ranking[None, :] == jnp.arange(picked_total, dtype=jnp.int32)[:, None]
    )
    chosen = jnp.sum(jnp.where(matches, block_ids[None, :], 0), axis=1)
    chosen_live = jnp.any(matches, axis=1)
    chosen_start = piece_position[chosen] * RESPONSE_BLOCK
    query_positions = own_position[slot_ordinal] * RESPONSE_BLOCK + jnp.arange(
        RESPONSE_BLOCK, dtype=jnp.int32
    )
    query_matrix = answer_queries[slot_ordinal]

    def one_batch(state_in, batch_data, query_matrix=query_matrix, query_positions=query_positions):
        picked, live_flags, starts_of = batch_data

        def take_in(state_now):
            key_rows = jnp.take(blocked_keys, picked, axis=0).reshape(
                batch_blocks * RESPONSE_BLOCK, heads_kv, HEAD_SIZE
            )
            value_rows = jnp.take(blocked_values, picked, axis=0).reshape(
                batch_blocks * RESPONSE_BLOCK, heads_kv, HEAD_SIZE
            )
            key_positions = (
                starts_of[:, None] + jnp.arange(RESPONSE_BLOCK, dtype=jnp.int32)[None, :]
            ).reshape(-1)
            key_live = jnp.repeat(live_flags, RESPONSE_BLOCK)
            seen = (key_live[None, :] & (key_positions[None, :] <= query_positions[:, None]))[
                :, None, None, :
            ]
            return absorb(state_now, score_block(query_matrix, key_rows), seen, value_rows)

        def keep_state(state_now):
            return state_now

        return (lax.cond(jnp.any(live_flags), take_in, keep_state, state_in), None)

    batch_inputs = (
        chosen.reshape(batch_count, batch_blocks),
        chosen_live.reshape(batch_count, batch_blocks),
        chosen_start.reshape(batch_count, batch_blocks),
    )
    new_state, unused_out = lax.scan(one_batch, answer_states[slot_ordinal], batch_inputs)
    updated = [new_state]
    finished = (tuple(updated), prompt_state)
    answer_states, prompt_state = finished
    answer_rows = jnp.concatenate([finish(state_item) for state_item in answer_states], axis=0)
    prompt_result = finish(prompt_state)
    prompt_out, answer_out = (
        lax.all_to_all(prompt_result, "head", split_axis=0, concat_axis=1, tiled=True),
        lax.all_to_all(answer_rows, "head", split_axis=0, concat_axis=1, tiled=True),
    )
    return (prompt_out, answer_out)


def solution(mesh):
    in_specs = (
        P("seq", "head"),
        P("seq", "head"),
        P("seq", "head"),
        P("seq", "head"),
        P("seq", "head"),
        P("seq", "head"),
        P(),
        P(),
    )
    out_specs = (P(("seq", "head"), None), P(("seq", "head"), None))
    return jax.shard_map(
        on_device, mesh=mesh, in_specs=in_specs, out_specs=out_specs, check_vma=False
    )
```

profile of v0, /device:TPU:18, one launch (start us, length us, event | category | flops | bytes accessed | tf_op | source)
XLA Modules:
  0.0 201.0 jit_solution(6942071327549159299)
XLA Ops:
  7.2 0.7 all-gather.3.cloned.1.call-update
  7.9 0.7 all-gather.5.cloned.1.call-update
  8.7 1.0 copy.61
  9.8 18.6 %all_gather.12 = bf16[512,512]{1,0:T(8,128)(2,1)} all-gather(bf16[32,512]{1,0:T(8,128)(2,1)} %param.17), channel_id=1, replica_groups=mesh['seq'=16,'head'=2] {'seq'}, dimensions={0}, use_global_device_ids=true | all-gather | bytes 557056 | tf_op jit(solution)/shard_map/all_gather | solution.py:95
  28.4 2.0 reshape.234
  30.4 24.3 %all_gather.13 = bf16[512,512]{1,0:T(8,128)(2,1)} all-gather(bf16[32,512]{1,0:T(8,128)(2,1)} %param.18), channel_id=1, replica_groups=mesh['seq'=16,'head'=2] {'seq'}, dimensions={0}, use_global_device_ids=true | all-gather | bytes 557056 | tf_op jit(solution)/shard_map/all_gather | solution.py:96
  54.7 2.0 reshape.235
  56.6 21.0 %while.37 = (s32[]{:T(128)}, f32[192,4,8]{0,2,1:T(8,128)S(1)}, f32[192,4,8]{0,2,1:T(8,128)S(1)}, f32[192,4,8,128]{3,0,2,1:T(8,128)S(1)}, f32[32,4,8]{0,2,1:T(8,1...) while((s32[]{:T(128)}, f32[192,4,8]{0,2,1:T(8,128)S(1)}, ...), condition=%wide.region_5.6_spmd.clone, body=%wide.region_0.5_spmd.clone.sunk | while | flops 957263104 | bytes 47417864 | solution.py:124
  56.6 0.6 dynamic_slice.50
  57.2 0.6 iota_add_fusion.5
  57.9 1.3 constant_dynamic-slice_fusion.5
  59.7 0.4 fusion.65
  60.1 0.5 fusion.67
  60.9 1.6 bitcast_reduce_fusion.2
  62.6 2.2 %fusion.63 = f32[192,4,8]{0,2,1:T(8,128)S(1)} fusion(f32[4,256,192,8]{1,2,3,0:T(8,128)S(1)} %get-tuple-element.626, f32[192,4,8]{0,2,1:T(8,128)S(1)} %select_maximum_fusion.4), kind=kLoop, calls=%fused_computation.9.clone.1 | loop fusion | flops 4712448 | bytes 6340608 | tf_op jit(solution)/shard_map/while/body/eval_jaxpr/reduce_sum | solution.py:43
  64.8 2.3 %bitcast_add_fusion.3 = f32[192,4,8,128]{3,0,2,1:T(8,128)S(1)} fusion(f32[192,4,8,128]{3,0,2,1:T(8,128)S(1)} %get-tuple-element.658, f32[4,256,192,8]{1,2,3,0:T(8,128)S(1)} %get-tuple-element.626, f32[192,4,8]{0,2,1:T(8,128)S(1)} %select_maximum_fusion.4, f32[192,4,8]{0,2,1:T(8,128)S(1)} %get-tuple-element.628, pred[]{:T(512)S(6)} %compare.3, ...), kind=kOutput, calls=%fused_computation.11.clone.1 | convolution fusion | flops 409731072 | bytes 12894209 | tf_op jit(solution)/shard_map/while/body/eval_jaxpr/rjgs,sjd->rjgd/dot_general | solution.py:44
  67.1 0.6 dynamic_slice.50
  67.7 0.6 iota_add_fusion.5
  68.4 1.4 constant_dynamic-slice_fusion.5
  70.2 0.4 fusion.65
  70.6 0.5 fusion.67
  71.4 1.6 bitcast_reduce_fusion.2
  73.1 2.2 %fusion.63 = f32[192,4,8]{0,2,1:T(8,128)S(1)} fusion(f32[4,256,192,8]{1,2,3,0:T(8,128)S(1)} %get-tuple-element.626, f32[192,4,8]{0,2,1:T(8,128)S(1)} %select_maximum_fusion.4), kind=kLoop, calls=%fused_computation.9.clone.1 | loop fusion | flops 4712448 | bytes 6340608 | tf_op jit(solution)/shard_map/while/body/eval_jaxpr/reduce_sum | solution.py:43
  75.3 2.3 %bitcast_add_fusion.3 = f32[192,4,8,128]{3,0,2,1:T(8,128)S(1)} fusion(f32[192,4,8,128]{3,0,2,1:T(8,128)S(1)} %get-tuple-element.658, f32[4,256,192,8]{1,2,3,0:T(8,128)S(1)} %get-tuple-element.626, f32[192,4,8]{0,2,1:T(8,128)S(1)} %select_maximum_fusion.4, f32[192,4,8]{0,2,1:T(8,128)S(1)} %get-tuple-element.628, pred[]{:T(512)S(6)} %compare.3, ...), kind=kOutput, calls=%fused_computation.11.clone.1 | convolution fusion | flops 409731072 | bytes 12894209 | tf_op jit(solution)/shard_map/while/body/eval_jaxpr/rjgs,sjd->rjgd/dot_general | solution.py:44
  77.6 1.3 divide_convert_fusion.1
  78.9 0.8 copy.42
  79.7 1.8 all_to_all.28
  81.5 4.3 %all-to-all-start = ((bf16[2,16,4096]{2,1,0:T(8,128)(2,1)}), bf16[2,16,4096]{2,1,0:T(8,128)(2,1)}, u32[]{:S(2)}, u32[]{:S(2)}) async-start(bf16[2,16,4096]{2,1,0:T(8,128)(2,1)} %all_to_all.28), calls=%async_computation | async-start | bytes 524288 | tf_op jit(solution)/shard_map/all_to_all | solution.py:188
  86.0 0.6 dynamic_slice.35
  86.5 1.3 fusion.44
  87.8 1.3 fusion.45
  90.5 0.7 convert_bitcast_fusion
  91.8 0.6 gather_fusion.2
  92.6 1.7 copy.62
  94.3 1.8 copy.45
  96.1 5.5 %reshape.241 = bf16[16,192,4,128]{3,2,1,0:T(4,128)(2,1)} reshape(bf16[3072,512]{1,0:T(8,128)(2,1)} %all-gather.3.cloned.1.call-done) | data formatting | bytes 6291456 | tf_op jit(solution)/shard_map/reshape | solution.py:131
  101.6 3.5 %all-gather.5.cloned.1.call-done = bf16[3072,512]{1,0:T(8,128)(2,1)} async-done(((bf16[192,512]{1,0:T(8,128)(2,1)}), bf16[3072,512]{1,0:T(8,128)(2,1)}) %all-gather.5.cloned.1.call-update) | async-done | bytes 3145744 | tf_op jit(solution)/shard_map/all_gather | solution.py:127
  105.1 5.5 %reshape.242 = bf16[16,192,4,128]{3,2,1,0:T(4,128)(2,1)} reshape(bf16[3072,512]{1,0:T(8,128)(2,1)} %all-gather.5.cloned.1.call-done) | data formatting | bytes 6291456 | tf_op jit(solution)/shard_map/reshape | solution.py:132
  110.6 62.2 %while.36 = (s32[]{:T(128)}, f32[192,4,8]{0,2,1:T(8,128)S(1)}, f32[192,4,8]{0,2,1:T(8,128)S(1)}, f32[192,4,8,128]{3,0,2,1:T(8,128)S(1)}, pred[2,4]{1,0:T(4,128)(...) while((s32[]{:T(128)}, f32[192,4,8]{0,2,1:T(8,128)S(1)}, ...), condition=%wide.region_20.22_spmd.clone, body=%wide.region_14.21_spmd.clone.sunk | while | flops 2470492160 | bytes 155146736 | solution.py:181
  110.6 0.7 fusion.59
  112.0 29.7 %conditional.3 = ((f32[192,4,8]{0,2,1:T(8,128)S(1)}, f32[192,4,8]{0,2,1:T(8,128)S(1)}, f32[192,4,8,128]{3,0,2,1:T(8,128)S(1)})) conditional(s32[]{:T(128)} %convert_element_type.62, (f32[192,4,8]{0,2,1:T(8,128)S(1)}, f32[192,4,8]{0,2,1:T(8,128)S(1)}, f32[192,4,8,128]{3,0,2,1:T(8,128)S(1)}) %tuple.83, (pred[1,4]{1,0:T(4,128)(4,1)S(1)}, ...), branch_computations={%region_16.16_spmd, %region_17.20_spmd} | conditional | flops 2470492160 | bytes 155145696 | solution.py:174
  112.4 3.9 %gather_fusion.1 = bf16[4,192,4,128]{3,2,1,0:T(4,128)(2,1)} fusion(bf16[16,192,4,128]{3,2,1,0:T(4,128)(2,1)} %get-tuple-element.205, s32[1024]{0:T(1024)S(1)} %pad_clamp_fusion), kind=kCustom, calls=%fused_computation.1.clone | custom fusion | bytes 1572880 | tf_op jit(solution)/shard_map/while/body/eval_jaxpr/cond/branch_1_fun/jit(_take)/gather | solution.py:159
  116.4 4.0 %gather_fusion = bf16[4,192,4,128]{3,2,1,0:T(4,128)(2,1)} fusion(bf16[16,192,4,128]{3,2,1,0:T(4,128)(2,1)} %get-tuple-element.200, s32[1024]{0:T(1024)S(1)} %pad_clamp_fusion), kind=kCustom, calls=%fused_computation.clone | custom fusion | bytes 1572880 | tf_op jit(solution)/shard_map/while/body/eval_jaxpr/cond/branch_1_fun/jit(_take)/gather | solution.py:156
  120.3 2.2 %broadcast_select_fusion = (bf16[4,192,4,128]{3,2,1,0:T(4,128)(2,1)S(1)}, bf16[4,192,4,128]{3,2,1,0:T(4,128)(2,1)S(1)}) fusion(bf16[4,192,4,128]{3,2,1,0:T(4,128)(2,1)} %gather_fusion.1, pred[4]{0:T(512)(128)(4,1)S(1)} %get-tuple-element.439, bf16[4,192,4,128]{3,2,1,0:T(4,128)(2,1)} %gather_fusion), kind=kLoop, calls=%fused_computation.59 | loop fusion | flops 786432 | bytes 3145732 | tf_op jit(solution)/shard_map/while/body/eval_jaxpr/cond/branch_1_fun/jit(_take)/select_n | solution.py:159
  122.7 3.5 %fusion.27 = (f32[192,4,8]{0,2,1:T(8,128)S(1)}, f32[4,768,192,8]{1,2,3,0:T(8,128)S(1)}) fusion(pred[192,768]{1,0:T(8,128)(4,1)S(1)} %compare_and_fusion, bf16[192,4,8,128]{3,0,2,1:T(8,128)(2,1)S(1)} %copy-done.2, bf16[768,4,128,1]{2,1,0,3:T(4,128)(2,1)S(1)} %bitcast.130), kind=kOutput, calls=%fused_computation.48 | convolution fusion | flops 1222109184 | bytes 21405696 | tf_op jit(solution)/shard_map/while/body/eval_jaxpr/cond/branch_1_fun/rjgd,sjd->rjgs/dot_general | solution.py:32
  126.3 5.4 %fusion.31 = f32[192,4,8]{0,2,1:T(8,128)S(1)} fusion(f32[4,768,192,8]{1,2,3,0:T(8,128)S(1)} %get-tuple-element.457, f32[192,4,8]{0,2,1:T(8,128)S(1)} %max.10, pred[192,768]{1,0:T(8,128)(4,1)S(1)} %compare_and_fusion), kind=kLoop, calls=%fused_computation.52 | loop fusion | flops 18868224 | bytes 19070976 | tf_op jit(solution)/shard_map/while/body/eval_jaxpr/cond/branch_1_fun/reduce_sum | solution.py:43
  131.7 1.1 copy-done
  132.7 9.0 %bitcast_add_fusion.1 = f32[192,4,8,128]{3,0,2,1:T(8,128)S(1)} fusion(f32[192,4,8,128]{3,0,2,1:T(8,128)S(1)} %get-tuple-element.204, f32[4,768,192,8]{1,2,3,0:T(8,128)} %copy-done, f32[192,4,8]{0,2,1:T(8,128)S(1)} %max.10, pred[192,768]{1,0:T(8,128)(4,1)S(1)} %compare_and_fusion, f32[192,4,8]{0,2,1:T(8,128)S(1)} %get-tuple-element.438, ...), kind=kOutput, calls=%fused_computation.55 | convolution fusion | flops 1228406784 | bytes 26148864 | tf_op jit(solution)/shard_map/while/body/eval_jaxpr/cond/branch_1_fun/rjgs,sjd->rjgd/dot_general | solution.py:44
  141.8 0.7 fusion.59
  143.2 29.7 %conditional.3 = ((f32[192,4,8]{0,2,1:T(8,128)S(1)}, f32[192,4,8]{0,2,1:T(8,128)S(1)}, f32[192,4,8,128]{3,0,2,1:T(8,128)S(1)})) conditional(s32[]{:T(128)} %convert_element_type.62, (f32[192,4,8]{0,2,1:T(8,128)S(1)}, f32[192,4,8]{0,2,1:T(8,128)S(1)}, f32[192,4,8,128]{3,0,2,1:T(8,128)S(1)}) %tuple.83, (pred[1,4]{1,0:T(4,128)(4,1)S(1)}, ...), branch_computations={%region_16.16_spmd, %region_17.20_spmd} | conditional | flops 2470492160 | bytes 155145696 | solution.py:174
  143.5 3.9 %gather_fusion.1 = bf16[4,192,4,128]{3,2,1,0:T(4,128)(2,1)} fusion(bf16[16,192,4,128]{3,2,1,0:T(4,128)(2,1)} %get-tuple-element.205, s32[1024]{0:T(1024)S(1)} %pad_clamp_fusion), kind=kCustom, calls=%fused_computation.1.clone | custom fusion | bytes 1572880 | tf_op jit(solution)/shard_map/while/body/eval_jaxpr/cond/branch_1_fun/jit(_take)/gather | solution.py:159
  147.5 4.0 %gather_fusion = bf16[4,192,4,128]{3,2,1,0:T(4,128)(2,1)} fusion(bf16[16,192,4,128]{3,2,1,0:T(4,128)(2,1)} %get-tuple-element.200, s32[1024]{0:T(1024)S(1)} %pad_clamp_fusion), kind=kCustom, calls=%fused_computation.clone | custom fusion | bytes 1572880 | tf_op jit(solution)/shard_map/while/body/eval_jaxpr/cond/branch_1_fun/jit(_take)/gather | solution.py:156
  151.4 2.2 %broadcast_select_fusion = (bf16[4,192,4,128]{3,2,1,0:T(4,128)(2,1)S(1)}, bf16[4,192,4,128]{3,2,1,0:T(4,128)(2,1)S(1)}) fusion(bf16[4,192,4,128]{3,2,1,0:T(4,128)(2,1)} %gather_fusion.1, pred[4]{0:T(512)(128)(4,1)S(1)} %get-tuple-element.439, bf16[4,192,4,128]{3,2,1,0:T(4,128)(2,1)} %gather_fusion), kind=kLoop, calls=%fused_computation.59 | loop fusion | flops 786432 | bytes 3145732 | tf_op jit(solution)/shard_map/while/body/eval_jaxpr/cond/branch_1_fun/jit(_take)/select_n | solution.py:159
  153.9 3.5 %fusion.27 = (f32[192,4,8]{0,2,1:T(8,128)S(1)}, f32[4,768,192,8]{1,2,3,0:T(8,128)S(1)}) fusion(pred[192,768]{1,0:T(8,128)(4,1)S(1)} %compare_and_fusion, bf16[192,4,8,128]{3,0,2,1:T(8,128)(2,1)S(1)} %copy-done.2, bf16[768,4,128,1]{2,1,0,3:T(4,128)(2,1)S(1)} %bitcast.130), kind=kOutput, calls=%fused_computation.48 | convolution fusion | flops 1222109184 | bytes 21405696 | tf_op jit(solution)/shard_map/while/body/eval_jaxpr/cond/branch_1_fun/rjgd,sjd->rjgs/dot_general | solution.py:32
  157.4 5.4 %fusion.31 = f32[192,4,8]{0,2,1:T(8,128)S(1)} fusion(f32[4,768,192,8]{1,2,3,0:T(8,128)S(1)} %get-tuple-element.457, f32[192,4,8]{0,2,1:T(8,128)S(1)} %max.10, pred[192,768]{1,0:T(8,128)(4,1)S(1)} %compare_and_fusion), kind=kLoop, calls=%fused_computation.52 | loop fusion | flops 18868224 | bytes 19070976 | tf_op jit(solution)/shard_map/while/body/eval_jaxpr/cond/branch_1_fun/reduce_sum | solution.py:43
  162.8 1.1 copy-done
  163.9 9.0 %bitcast_add_fusion.1 = f32[192,4,8,128]{3,0,2,1:T(8,128)S(1)} fusion(f32[192,4,8,128]{3,0,2,1:T(8,128)S(1)} %get-tuple-element.204, f32[4,768,192,8]{1,2,3,0:T(8,128)} %copy-done, f32[192,4,8]{0,2,1:T(8,128)S(1)} %max.10, pred[192,768]{1,0:T(8,128)(4,1)S(1)} %compare_and_fusion, f32[192,4,8]{0,2,1:T(8,128)S(1)} %get-tuple-element.438, ...), kind=kOutput, calls=%fused_computation.55 | convolution fusion | flops 1228406784 | bytes 26148864 | tf_op jit(solution)/shard_map/while/body/eval_jaxpr/cond/branch_1_fun/rjgs,sjd->rjgd/dot_general | solution.py:44
  172.9 1.0 divide_convert_fusion
  173.9 1.0 copy.46
  174.9 2.1 %all_to_all.32 = bf16[2,96,4096]{2,1,0:T(8,128)(2,1)} reshape(bf16[192,4,8,128]{3,2,1,0:T(8,128)(2,1)S(1)} %copy.46) | data formatting | bytes 3145728 | tf_op jit(solution)/shard_map/all_to_all | solution.py:189
  177.0 3.7 %all-to-all-start.1 = ((bf16[2,96,4096]{2,1,0:T(8,128)(2,1)}), bf16[2,96,4096]{2,1,0:T(8,128)(2,1)S(1)}, u32[]{:S(2)}, u32[]{:S(2)}) async-start(bf16[2,96,4096]{2,1,0:T(8,128)(2,1)} %all_to_all.32), calls=%async_computation.1 | async-start | bytes 3145728 | tf_op jit(solution)/shard_map/all_to_all | solution.py:189
  180.6 1.7 copy.59
  182.3 10.5 %all-to-all-done.1 = bf16[2,96,4096]{2,1,0:T(8,128)(2,1)S(1)} async-done(((bf16[2,96,4096]{2,1,0:T(8,128)(2,1)}), bf16[2,96,4096]{2,1,0:T(8,128)(2,1)S(1)}, u32[]{:S(2)}, u32[]{:S(2)}) %all-to-all-start.1) | async-done | bytes 1572896 | tf_op jit(solution)/shard_map/all_to_all | solution.py:189
  192.8 1.3 copy.60
  (94 shorter events, 4.1 us)
Async XLA Ops:
  7.2 88.9 %all-gather.3.cloned.1.call-start = ((), (), s32[]{:S(2)}) async-start(), calls=%async_computation.2 | async-start | bytes 3342336 | tf_op jit(solution)/shard_map/all_gather | solution.py:126
  7.9 97.2 %all-gather.5.cloned.1.call-start = ((), (), s32[]{:S(2)}) async-start(), calls=%async_computation.3 | async-start | bytes 3342336 | tf_op jit(solution)/shard_map/all_gather | solution.py:127
  56.6 29.1 %copy-start.5 = (s32[4]{0:T(128)S(1)}, s32[4]{0:T(128)}, u32[]{:S(2)}) copy-start(s32[4]{0:T(128)} %param.22) | copy-start | bytes 52
  56.6 29.3 %copy-start.6 = (s32[16]{0:T(128)S(1)}, s32[16]{0:T(128)}, u32[]{:S(2)}) copy-start(s32[16]{0:T(128)} %param.23) | copy-start | bytes 196
  56.6 3.4 %copy-start.3 = (f32[32,4,8,128]{3,0,2,1:T(8,128)S(1)}, f32[32,4,8,128]{3,0,2,1:T(8,128)}, u32[]{:S(2)}) copy-start(f32[32,4,8,128]{3,0,2,1:T(8,128)} %get-tuple-element.661) | copy-start | bytes 1572868 | tf_op jit(solution)/shard_map/while
  57.9 2.7 %copy-start.1 = (bf16[192,4096]{1,0:T(8,128)(2,1)S(1)}, bf16[192,4096]{1,0:T(8,128)(2,1)}, u32[]{:S(2)}) copy-start(bf16[192,4096]{1,0:T(8,128)(2,1)} %get-tuple-element.678) | copy-start | bytes 4718596 | tf_op jit(solution)/shard_map/while
  60.6 2.0 copy-start.4
  67.1 3.5 %copy-start.3 = (f32[32,4,8,128]{3,0,2,1:T(8,128)S(1)}, f32[32,4,8,128]{3,0,2,1:T(8,128)}, u32[]{:S(2)}) copy-start(f32[32,4,8,128]{3,0,2,1:T(8,128)} %get-tuple-element.661) | copy-start | bytes 1572868 | tf_op jit(solution)/shard_map/while
  68.4 2.7 %copy-start.1 = (bf16[192,4096]{1,0:T(8,128)(2,1)S(1)}, bf16[192,4096]{1,0:T(8,128)(2,1)}, u32[]{:S(2)}) copy-start(bf16[192,4096]{1,0:T(8,128)(2,1)} %get-tuple-element.678) | copy-start | bytes 4718596 | tf_op jit(solution)/shard_map/while
  71.1 2.0 copy-start.4
  81.5 95.5 %all-to-all-start = ((bf16[2,16,4096]{2,1,0:T(8,128)(2,1)}), bf16[2,16,4096]{2,1,0:T(8,128)(2,1)}, u32[]{:S(2)}, u32[]{:S(2)}) async-start(bf16[2,16,4096]{2,1,0:T(8,128)(2,1)} %all_to_all.28), calls=%async_computation | async-start | bytes 524288 | tf_op jit(solution)/shard_map/all_to_all | solution.py:188
  120.3 2.4 %copy-start.2 = (bf16[192,4,8,128]{3,0,2,1:T(8,128)(2,1)S(1)}, bf16[192,4,8,128]{3,0,2,1:T(8,128)(2,1)}, u32[]{:S(2)}) copy-start(bf16[192,4,8,128]{3,0,2,1:T(8,128)(2,1)} %get-tuple-element.202) | copy-start | bytes 4718596 | tf_op jit(solution)/shard_map/while/body/eval_jaxpr/cond
  126.2 6.5 %copy-start = (f32[4,768,192,8]{1,2,3,0:T(8,128)}, f32[4,768,192,8]{1,2,3,0:T(8,128)S(1)}, u32[]{:S(2)}) copy-start(f32[4,768,192,8]{1,2,3,0:T(8,128)S(1)} %get-tuple-element.457) | copy-start | bytes 56623108 | tf_op jit(solution)/shard_map/while/body/eval_jaxpr/cond
  151.4 2.4 %copy-start.2 = (bf16[192,4,8,128]{3,0,2,1:T(8,128)(2,1)S(1)}, bf16[192,4,8,128]{3,0,2,1:T(8,128)(2,1)}, u32[]{:S(2)}) copy-start(bf16[192,4,8,128]{3,0,2,1:T(8,128)(2,1)} %get-tuple-element.202) | copy-start | bytes 4718596 | tf_op jit(solution)/shard_map/while/body/eval_jaxpr/cond
  157.4 6.5 %copy-start = (f32[4,768,192,8]{1,2,3,0:T(8,128)}, f32[4,768,192,8]{1,2,3,0:T(8,128)S(1)}, u32[]{:S(2)}) copy-start(f32[4,768,192,8]{1,2,3,0:T(8,128)S(1)} %get-tuple-element.457) | copy-start | bytes 56623108 | tf_op jit(solution)/shard_map/while/body/eval_jaxpr/cond
  177.0 15.9 %all-to-all-start.1 = ((bf16[2,96,4096]{2,1,0:T(8,128)(2,1)}), bf16[2,96,4096]{2,1,0:T(8,128)(2,1)S(1)}, u32[]{:S(2)}, u32[]{:S(2)}) async-start(bf16[2,96,4096]{2,1,0:T(8,128)(2,1)} %all_to_all.32), calls=%async_computation.1 | async-start | bytes 3145728 | tf_op jit(solution)/shard_map/all_to_all | solution.py:189
Sparse Core Ops, SparseCore 0:
  10.3 48.7 all-gather.2
  61.3 43.7 all-gather.4
where the time goes:
time: 205 us; the launch traced here: 201 us
  local copies, waits for them, and re-layouts  52.8 us (26%)
  blocking collectives  42.8 us (21%)
  matrix products  34.5 us (17%)
  other arithmetic  30.1 us (15%)
  waiting for transfers between devices  15.4 us (8%)
  between operations  15.4 us (8%)
  starting transfers between devices  8.04 us (4%)
    all_gather x1, blocking collectives, on_device(): piece_value = lax.all_gather(prompt_token_value, 'seq', axis=0, tiled=True)  24.3 us
    dot_general x6, matrix products, absorb(): jnp.einsum('rjgs,sjd->rjgd', weights.astype(jnp.bfloat16), value_rows, pr...  23.4 us
    all_gather x1, blocking collectives, on_device(): piece_key = lax.all_gather(prompt_token_key, 'seq', axis=0, tiled=True)  18.6 us
    reduce_sum x6, other arithmetic, absorb(): total_new = total_old * factor + jnp.sum(weights, axis=-1)  15.9 us
    dot_general x6, matrix products, score_block(): jnp.einsum('rjgd,sjd->rjgs', query_matrix, key_rows, preferred_element_ty...  11 us
    all_to_all x1, waiting for transfers between devices, on_device(): lax.all_to_all(answer_rows, 'head', split_axis=0, concat_axis=1, tiled=True)  10.5 us
    gather x2, local copies, waits for them, and re-layouts, take_in(): jnp.take(blocked_keys, picked, axis=0)  7.93 us
    gather x2, local copies, waits for them, and re-layouts, take_in(): jnp.take(blocked_values, picked, axis=0)  7.87 us
  transfers between devices with their start and end apart: 4, of which 2 were waited for; matrix products, arithmetic and copies ran while one was open for 55% of the time, Pallas kernels for 0%

commit v1 on v0

v1 whole, which is shorter than its diff:
```python
import functools
import math

import jax
import jax.numpy as jnp
from jax import lax
from jax.experimental import pallas as pl
from jax.experimental.pallas import tpu as pltpu
from jax.sharding import PartitionSpec as P

HEAD_SIZE = 128
RESPONSE_BLOCK = 192
NEG_FILL = -1e30
MESH = pl.DeviceIdType.MESH
SCALE = HEAD_SIZE ** (-0.5) * math.log2(math.e)


def nearest_first(count):
    order = []
    for step in range(1, count // 2 + 1):
        order.append(step)
        if count - step != step:
            order.append(count - step)
    return order


def softmax_step(state, scores, value_rows):
    peak = jnp.max(scores, axis=-1, keepdims=True)
    if state is not None:
        peak = jnp.maximum(state[0], peak)
    weights = jnp.exp2(scores - peak)
    total = jnp.sum(weights, axis=-1, keepdims=True)
    mixed = jnp.dot(weights.astype(jnp.bfloat16), value_rows, preferred_element_type=jnp.float32)
    if state is not None:
        factor = jnp.exp2(state[0] - peak)
        total = state[1] * factor + total
        mixed = state[2] * factor + mixed
    return (peak, total, mixed)


def score(query_rows, key_rows):
    return (
        lax.dot_general(
            query_rows, key_rows, (((1,), (1,)), ((), ())), preferred_element_type=jnp.float32
        )
        * SCALE
    )


def kernel(
    seq_count, head_count, heads_kv, group, most, chunk,
    lengths_ref, table_ref, pq_hbm, pk_hbm, pv_hbm, rq_hbm, rk_hbm, rv_hbm,
    pout_ref, aout_ref,
    *scratch,
):
    pieces = scratch[:heads_kv]
    stage_a = scratch[heads_kv:2 * heads_kv]
    stage_p = scratch[2 * heads_kv:3 * heads_kv]
    (keys, values, queries, pqueries, pack_sem, q_sem, recv_sem, z_sem, x_sem, c_sem,
     out_send, out_recv, out_local) = scratch[3 * heads_kv:]
    prompt_rows = pq_hbm.shape[0]
    block = rq_hbm.shape[0]
    prompt_total = prompt_rows * seq_count
    width = group * HEAD_SIZE
    z_count = seq_count // 4
    me = lax.axis_index("seq")
    head = lax.axis_index("head")
    z, x, c = me // 4, (me // 2) % 2, me % 2

    def place(zi, xi, ci):
        return zi * 4 + xi * 2 + ci

    x_peer, c_peer = place(z, 1 - x, c), place(z, x, 1 - c)
    offsets = nearest_first(z_count)

    packs = []
    for j in range(heads_kv):
        cols = pl.ds(j * HEAD_SIZE, HEAD_SIZE)
        row = 0
        for k, source in enumerate((rk_hbm, rv_hbm, pk_hbm, pv_hbm)):
            rows = source.shape[0]
            copy = pltpu.make_async_copy(
                source.at[:, cols], pieces[j].at[me, pl.ds(row, rows), :], pack_sem.at[j, k]
            )
            copy.start()
            packs.append(copy)
            row += rows
    q_copies = [
        pltpu.make_async_copy(rq_hbm, queries, q_sem.at[0]),
        pltpu.make_async_copy(pq_hbm, pqueries, q_sem.at[1]),
    ]
    for copy in q_copies:
        copy.start()

    barrier = pltpu.get_barrier_semaphore()
    peers = [(place((z + k) % z_count, x, c), head) for k in range(1, z_count)]
    peers += [(x_peer, head), (c_peer, head)]
    peers += [(me, (head + k) % head_count) for k in range(1, head_count)]
    for peer in peers:
        pl.semaphore_signal(barrier, inc=1, device_id=peer, device_id_type=MESH)
    pl.semaphore_wait(barrier, len(peers))

    sends = []

    def send(j, source, target, sem):
        copy = pltpu.make_async_remote_copy(
            src_ref=pieces[j].at[source], dst_ref=pieces[j].at[source],
            send_sem=sem, recv_sem=recv_sem.at[j, source],
            device_id=(target, head), device_id_type=MESH,
        )
        copy.start()
        sends.append((j, copy))

    def arrived(j, source):
        pltpu.make_async_remote_copy(
            src_ref=pieces[j].at[source], dst_ref=pieces[j].at[source],
            send_sem=c_sem.at[j, 0, 0], recv_sem=recv_sem.at[j, source],
            device_id=(c_peer, head), device_id_type=MESH,
        ).wait_recv()

    def x_own(j):
        if j < heads_kv:
            send(j, me, x_peer, x_sem.at[j, 0])

    def forward_z(j, k):
        if j < heads_kv:
            source = place((z + z_count - offsets[k]) % z_count, x, c)
            arrived(j, source)
            send(j, source, x_peer, x_sem.at[j, offsets[k]])
            send(j, source, c_peer, c_sem.at[j, 0, offsets[k]])

    def forward_x(j):
        if j < heads_kv:
            for k in [0] + offsets:
                source = place((z + z_count - k) % z_count, 1 - x, c)
                arrived(j, source)
                send(j, source, c_peer, c_sem.at[j, 1, k])

    def wait_c(j):
        for xi in range(2):
            for zi in range(z_count):
                arrived(j, place(zi, xi, 1 - c))

    for j in range(heads_kv):
        for copy in packs[4 * j:4 * j + 4]:
            copy.wait()
        for k in offsets:
            send(j, me, place((z + k) % z_count, x, c), z_sem.at[j, k])
        if j == 0:
            x_own(0)
        send(j, me, c_peer, c_sem.at[j, 0, 0])
    x_own(1)

    own = table_ref[me]
    first = jnp.int32(0)
    bound = jnp.int32(0)
    for m in range(lengths_ref.shape[0]):
        bound = bound + lengths_ref[m]
        first = jnp.where(own >= bound, bound, first)
    base = prompt_total + (own - first) * block
    slots = []
    for p in range(most):
        wanted = first + p
        slots.append(
            lax.fori_loop(
                0, seq_count,
                lambda s, a, wanted=wanted: jnp.where(table_ref[s] == wanted, s, a),
                jnp.int32(0),
            )
        )

    for k in range(len(offsets)):
        forward_z(0, k)
    forward_x(0)
    for copy in q_copies:
        copy.wait()

    total_keys = prompt_total + most * block
    bounds = [(0, prompt_total)]
    at = prompt_total
    while at < total_keys:
        bounds.append((at, min(chunk, total_keys - at)))
        at += bounds[-1][1]
    pair = 2
    steps = group // pair
    out_copies = []

    for j in range(heads_kv):
        wait_c(j)
        for s in range(seq_count):
            rows = pl.ds(s * prompt_rows, prompt_rows)
            keys[rows, :] = pieces[j][s, 2 * block:2 * block + prompt_rows, :]
            values[rows, :] = pieces[j][s, 2 * block + prompt_rows:2 * (block + prompt_rows), :]
        for p in range(most):
            rows = pl.ds(prompt_total + p * block, block)
            keys[rows, :] = pieces[j][slots[p], 0:block, :]
            values[rows, :] = pieces[j][slots[p], block:2 * block, :]

        query = jnp.concatenate(
            [pqueries[:, (j * group + g) * HEAD_SIZE:(j * group + g + 1) * HEAD_SIZE] for g in range(group)],
            axis=0,
        )
        scores = score(query, keys[0:prompt_total, :])
        key_at = lax.broadcasted_iota(jnp.int32, scores.shape, 1)
        query_at = me * prompt_rows + lax.broadcasted_iota(jnp.int32, scores.shape, 0) % prompt_rows
        scores = jnp.where(key_at <= query_at, scores, NEG_FILL)
        state = softmax_step(None, scores, values[0:prompt_total, :])
        out = (state[2] / state[1]).astype(jnp.bfloat16)
        part = prompt_rows // head_count
        for g in range(group):
            for h in range(head_count):
                stage_p[j][h, :, g * HEAD_SIZE:(g + 1) * HEAD_SIZE] = out[
                    g * prompt_rows + h * part:g * prompt_rows + (h + 1) * part, :
                ]

        def step(i, carry, j=j):
            for k in range(len(offsets)):
                if k < steps - 1:
                    last = len(offsets) if k == steps - 2 else k + 1

                    @pl.when(i == k + 1)
                    def _(k=k, last=last):
                        for kk in range(k, last):
                            forward_z(j + 1, kk)
                        if k == min(len(offsets), steps - 1) - 1:
                            x_own(j + 2)
            states = [None] * pair
            rows_of = []
            for u in range(pair):
                cols = pl.ds(pl.multiple_of((j * group + i * pair + u) * HEAD_SIZE, HEAD_SIZE), HEAD_SIZE)
                rows_of.append(queries[:, cols])
            for n, (start, size) in enumerate(bounds):
                for u in range(pair):
                    scores = score(rows_of[u], keys[start:start + size, :])
                    if start >= prompt_total:
                        gap = lax.broadcasted_iota(jnp.int32, scores.shape, 1) - lax.broadcasted_iota(
                            jnp.int32, scores.shape, 0
                        )
                        scores = jnp.where(gap <= base - start, scores, NEG_FILL)
                    states[u] = softmax_step(states[u], scores, values[start:start + size, :])
            share = block // head_count
            for u in range(pair):
                out = (states[u][2] / states[u][1]).astype(jnp.bfloat16)
                cols = pl.ds(pl.multiple_of((i * pair + u) * HEAD_SIZE, HEAD_SIZE), HEAD_SIZE)
                for h in range(head_count):
                    stage_a[j][h, :, cols] = out[h * share:(h + 1) * share, :]
            return carry

        lax.fori_loop(0, steps, step, 0)
        forward_x(j + 1)

        cols = pl.ds(pl.multiple_of((head * heads_kv + j) * width, width), width)
        for n, (staged, result) in enumerate(((stage_a[j], aout_ref), (stage_p[j], pout_ref))):
            for k in range(1, head_count):
                target = (head + k) % head_count
                copy = pltpu.make_async_remote_copy(
                    src_ref=staged.at[target], dst_ref=result.at[:, cols],
                    send_sem=out_send.at[j, n, k], recv_sem=out_recv.at[j, n, head],
                    device_id=(me, target), device_id_type=MESH,
                )
                copy.start()
                sends.append((j, copy))
            local = pltpu.make_async_copy(staged.at[head], result.at[:, cols], out_local.at[j, n])
            local.start()
            out_copies.append(local)

    for local in out_copies:
        local.wait()
    for j in range(heads_kv):
        for k in range(1, head_count):
            other = (head + k) % head_count
            cols = pl.ds(pl.multiple_of((other * heads_kv + j) * width, width), width)
            for n, (staged, result) in enumerate(((stage_a[j], aout_ref), (stage_p[j], pout_ref))):
                pltpu.make_async_remote_copy(
                    src_ref=staged.at[other], dst_ref=result.at[:, cols],
                    send_sem=out_send.at[j, n, k], recv_sem=out_recv.at[j, n, other],
                    device_id=(me, other), device_id_type=MESH,
                ).wait_recv()
    for j in range(heads_kv):
        for k in offsets:
            wait_sent(pieces[j].at[me], z_sem.at[j, k], c_peer, head)
        for k in range(z_count):
            wait_sent(pieces[j].at[me], x_sem.at[j, k], c_peer, head)
            for n in range(2):
                wait_sent(pieces[j].at[me], c_sem.at[j, n, k], c_peer, head)
        for n, staged in enumerate((stage_a[j], stage_p[j])):
            for k in range(1, head_count):
                wait_sent(staged.at[0], out_send.at[j, n, k], c_peer, head)


def wait_sent(ref, sem, peer, head):
    pltpu.make_async_remote_copy(
        src_ref=ref, dst_ref=ref, send_sem=sem, recv_sem=sem,
        device_id=(peer, head), device_id_type=MESH,
    ).wait_send()


def on_device(mesh_shape, pq, pk, pv, rq, rk, rv, lengths, table):
    seq_count, head_count = mesh_shape["seq"], mesh_shape["head"]
    heads_kv = rk.shape[1] // HEAD_SIZE
    group = rq.shape[1] // rk.shape[1]
    block, prompt_rows = rq.shape[0], pq.shape[0]
    most = table.shape[0] // 2
    width = group * HEAD_SIZE
    z_count = seq_count // 4
    total = prompt_rows * seq_count + most * block
    dma = pltpu.SemaphoreType.DMA
    any_space = pl.BlockSpec(memory_space=pl.ANY)
    smem = pl.BlockSpec(memory_space=pltpu.SMEM)
    vmem = pl.BlockSpec(memory_space=pltpu.VMEM)
    return pl.pallas_call(
        functools.partial(kernel, seq_count, head_count, heads_kv, group, most, 512),
        out_shape=(
            jax.ShapeDtypeStruct((prompt_rows // head_count, rq.shape[1] * head_count), jnp.bfloat16),
            jax.ShapeDtypeStruct((block // head_count, rq.shape[1] * head_count), jnp.bfloat16),
        ),
        in_specs=[smem] * 2 + [any_space] * 6,
        out_specs=(vmem, vmem),
        scratch_shapes=(
            [pltpu.VMEM((seq_count, 2 * (block + prompt_rows), HEAD_SIZE), jnp.bfloat16)] * heads_kv
            + [pltpu.VMEM((head_count, block // head_count, width), jnp.bfloat16)] * heads_kv
            + [pltpu.VMEM((head_count, prompt_rows // head_count, width), jnp.bfloat16)] * heads_kv
            + [
                pltpu.VMEM((total, HEAD_SIZE), jnp.bfloat16),
                pltpu.VMEM((total, HEAD_SIZE), jnp.bfloat16),
                pltpu.VMEM(rq.shape, jnp.bfloat16),
                pltpu.VMEM(pq.shape, jnp.bfloat16),
                dma((heads_kv, 4)),
                dma((2,)),
                dma((heads_kv, seq_count)),
                dma((heads_kv, z_count)),
                dma((heads_kv, z_count)),
                dma((heads_kv, 2, z_count)),
                dma((heads_kv, 2, head_count)),
                dma((heads_kv, 2, head_count)),
                dma((heads_kv, 2)),
            ]
        ),
        compiler_params=pltpu.CompilerParams(
            collective_id=0, has_side_effects=True, vmem_limit_bytes=60 * 1024 * 1024
        ),
    )(lengths, table, pq, pk, pv, rq, rk, rv)


def solution(mesh):
    sharded = P("seq", "head")
    out = P(("seq", "head"), None)
    return jax.shard_map(
        functools.partial(on_device, dict(mesh.shape)), mesh=mesh,
        in_specs=(sharded,) * 6 + (P(), P()), out_specs=(out, out), check_vma=False,
    )
```

time: 205 us -> 95.3 us (0.46)
  the two profiles are of different devices: /device:TPU:18 before, /device:TPU:0 now
where the time goes in v1:
time: 95.3 us; the launch traced here: 95.1 us
  Pallas kernels  90.1 us (95%)
  local copies, waits for them, and re-layouts  4.32 us (5%)
    pallas_call x1, Pallas kernels, on_device(): pl.pallas_call(functools.partial(kernel, seq_count, head_count, heads_kv,...  90.1 us
    unnamed x2, local copies, waits for them, and re-layouts  4.32 us

profile of v1, /device:TPU:0, one launch (start us, length us, event | category | flops | bytes accessed | tf_op | source)
XLA Modules:
  0.0 95.1 jit_solution(5185083443752285944)
XLA Ops:
  0.6 90.1 %shard_map.95 = (bf16[16,8192]{1,0:T(8,128)(2,1)}, bf16[96,8192]{1,0:T(8,128)(2,1)}) custom-call(s32[4]{0:T(128)} %lengths_ref.1, s32[16]{0:T(128)} %table_ref.1, bf16[32,4096]{1,0:T(8,128)(2,1)} %pq_hbm.1, bf16[32,512]{1,0:T(8,128)(2,1)} %pk_hbm.1, bf16[32,512]{1,0:T(8,128)(2,1)} %pv_hbm.1, bf16[192,4096]{1,0:T(8,128)(2,1)} %rq_hbm.1, ...), custom_call_target="tpu_custom_call" | custom-call | tf_op jit(solution)/shard_map/pallas_call | solution.py:311
  90.8 1.7 %copy.12 = bf16[16,8192]{1,0:T(8,128)(2,1)} copy(bf16[16,8192]{1,0:T(8,128)(2,1)} %get-tuple-element.4) | data formatting | bytes 524288
  92.4 2.7 %copy.13 = bf16[96,8192]{1,0:T(8,128)(2,1)} copy(bf16[96,8192]{1,0:T(8,128)(2,1)} %get-tuple-element.5) | data formatting | bytes 3145728

commit v2 on v1

--- a/solution.py
+++ b/solution.py
@@ -57,7 +57,8 @@
     stage_a = scratch[heads_kv:2 * heads_kv]
     stage_p = scratch[2 * heads_kv:3 * heads_kv]
     (keys, values, queries, pqueries, pack_sem, q_sem, recv_sem, z_sem, x_sem, c_sem,
-     out_send, out_recv, out_local) = scratch[3 * heads_kv:]
+     out_send, out_recv, out_local, bias, *rest) = scratch[3 * heads_kv:]
+    score_bufs, peaks = rest[:2], rest[2:]
     prompt_rows = pq_hbm.shape[0]
     block = rq_hbm.shape[0]
     prompt_total = prompt_rows * seq_count
@@ -67,11 +68,27 @@
     head = lax.axis_index("head")
     z, x, c = me // 4, (me // 2) % 2, me % 2
 
+    def z_source_offset(k):
+        if relayed:
+            return (z + 4 - z_source(k)) % 4
+        return offsets[k]
+
     def place(zi, xi, ci):
         return zi * 4 + xi * 2 + ci
 
     x_peer, c_peer = place(z, 1 - x, c), place(z, x, 1 - c)
     offsets = nearest_first(z_count)
+    relayed = z_count == 4
+    inner = jnp.where((z == 1) | (z == 2), 1, 0)
+
+    def mirrored(t):
+        return jnp.where(z < 2, t, 3 - t)
+
+    def z_source(k):
+        if relayed:
+            return mirrored((inner + 1 + k) % 4)
+        return (z + z_count - offsets[k]) % z_count
+
 
     packs = []
     for j in range(heads_kv):
@@ -124,14 +141,19 @@
 
     def forward_z(j, k):
         if j < heads_kv:
-            source = place((z + z_count - offsets[k]) % z_count, x, c)
+            source = place(z_source(k), x, c)
             arrived(j, source)
+            if relayed and k < 2:
+                @pl.when(inner == 1)
+                def _():
+                    send(j, source, place(mirrored(0), x, c), z_sem.at[j, 2 + k])
             send(j, source, x_peer, x_sem.at[j, offsets[k]])
             send(j, source, c_peer, c_sem.at[j, 0, offsets[k]])
 
-    def forward_x(j):
+    def forward_x(j, half):
         if j < heads_kv:
-            for k in [0] + offsets:
+            arrivals = [0] + [z_source_offset(k) for k in range(len(offsets))]
+            for k in arrivals[:len(arrivals) // 2] if half == 0 else arrivals[len(arrivals) // 2:]:
                 source = place((z + z_count - k) % z_count, 1 - x, c)
                 arrived(j, source)
                 send(j, source, c_peer, c_sem.at[j, 1, k])
@@ -144,12 +166,15 @@
     for j in range(heads_kv):
         for copy in packs[4 * j:4 * j + 4]:
             copy.wait()
-        for k in offsets:
-            send(j, me, place((z + k) % z_count, x, c), z_sem.at[j, k])
+        if relayed:
+            send(j, me, place(mirrored(1 - inner), x, c), z_sem.at[j, 0])
+            send(j, me, place(mirrored(2), x, c), z_sem.at[j, 1])
+        else:
+            for k in offsets:
+                send(j, me, place((z + k) % z_count, x, c), z_sem.at[j, k])
         if j == 0:
             x_own(0)
         send(j, me, c_peer, c_sem.at[j, 0, 0])
-    x_own(1)
 
     own = table_ref[me]
     first = jnp.int32(0)
@@ -157,7 +182,6 @@
     for m in range(lengths_ref.shape[0]):
         bound = bound + lengths_ref[m]
         first = jnp.where(own >= bound, bound, first)
-    base = prompt_total + (own - first) * block
     slots = []
     for p in range(most):
         wanted = first + p
@@ -169,9 +193,16 @@
             )
         )
 
+    for start in range(0, most * block, block):
+        gap = lax.broadcasted_iota(jnp.int32, (block, block), 1) - lax.broadcasted_iota(
+            jnp.int32, (block, block), 0
+        )
+        bias[:, start:start + block] = jnp.where(gap <= (own - first) * block - start, 0.0, NEG_FILL)
     for k in range(len(offsets)):
         forward_z(0, k)
-    forward_x(0)
+    x_own(1)
+    forward_x(0, 0)
+    forward_x(0, 1)
     for copy in q_copies:
         copy.wait()
 
@@ -183,7 +214,36 @@
         at += bounds[-1][1]
     pair = 2
     steps = group // pair
-    out_copies = []
+
+    part_width = pair * HEAD_SIZE
+
+    def out_refs(j, i, owner):
+        wide = part_width
+        if isinstance(i, int) and i == steps:
+            staged, result, start, wide = stage_p[j], pout_ref, 0, width
+        else:
+            staged, result, start = stage_a[j], aout_ref, i * part_width
+        start = start if isinstance(start, int) else pl.multiple_of(start, part_width)
+        cols = pl.ds(pl.multiple_of((owner * heads_kv + j) * width + start, wide), wide)
+        return staged, result.at[:, cols], pl.ds(start, wide)
+
+    def out_remote(j, i, k, owner):
+        target = (head + k) % head_count
+        staged, result, cols = out_refs(j, i, owner)
+        return pltpu.make_async_remote_copy(
+            src_ref=staged.at[target, :, cols], dst_ref=result,
+            send_sem=out_send.at[j, i, k], recv_sem=out_recv.at[j, i, owner],
+            device_id=(me, target), device_id_type=MESH,
+        )
+
+    def out_copy(j, i):
+        staged, result, cols = out_refs(j, i, head)
+        return pltpu.make_async_copy(staged.at[head, :, cols], result, out_local.at[j, i])
+
+    def send_out(j, i):
+        for k in range(1, head_count):
+            out_remote(j, i, k, head).start()
+        out_copy(j, i).start()
 
     for j in range(heads_kv):
         wait_c(j)
@@ -213,79 +273,116 @@
                     g * prompt_rows + h * part:g * prompt_rows + (h + 1) * part, :
                 ]
 
-        def step(i, carry, j=j):
-            for k in range(len(offsets)):
-                if k < steps - 1:
-                    last = len(offsets) if k == steps - 2 else k + 1
-
-                    @pl.when(i == k + 1)
-                    def _(k=k, last=last):
-                        for kk in range(k, last):
-                            forward_z(j + 1, kk)
-                        if k == min(len(offsets), steps - 1) - 1:
-                            x_own(j + 2)
-            states = [None] * pair
-            rows_of = []
-            for u in range(pair):
-                cols = pl.ds(pl.multiple_of((j * group + i * pair + u) * HEAD_SIZE, HEAD_SIZE), HEAD_SIZE)
-                rows_of.append(queries[:, cols])
-            for n, (start, size) in enumerate(bounds):
-                for u in range(pair):
-                    scores = score(rows_of[u], keys[start:start + size, :])
-                    if start >= prompt_total:
-                        gap = lax.broadcasted_iota(jnp.int32, scores.shape, 1) - lax.broadcasted_iota(
-                            jnp.int32, scores.shape, 0
-                        )
-                        scores = jnp.where(gap <= base - start, scores, NEG_FILL)
-                    states[u] = softmax_step(states[u], scores, values[start:start + size, :])
+        def first_pass(g, u):
+            cols = pl.ds(pl.multiple_of((j * group + g) * HEAD_SIZE, HEAD_SIZE), HEAD_SIZE)
+            query = queries[:, cols]
+            peak = None
+            for start, size in bounds:
+                raw = lax.dot_general(
+                    query, keys[start:start + size, :], (((1,), (1,)), ((), ())),
+                    preferred_element_type=jnp.float32,
+                )
+                if start >= prompt_total:
+                    raw = raw + bias[:, start - prompt_total:start - prompt_total + size]
+                score_bufs[u][:, start:start + size] = raw
+                for lane in range(0, size, HEAD_SIZE):
+                    strip = raw[:, lane:lane + HEAD_SIZE]
+                    peak = strip if peak is None else jnp.maximum(peak, strip)
+            peaks[u][...] = peak
+
+        def second_pass(g, u):
+            peak = jnp.max(peaks[u][...], axis=-1, keepdims=True) * SCALE
+            total = mixed = None
+            for start, size in bounds:
+                weights = jnp.exp2(score_bufs[u][:, start:start + size] * SCALE - peak)
+                for lane in range(0, size, HEAD_SIZE):
+                    strip = weights[:, lane:lane + HEAD_SIZE]
+                    total = strip if total is None else total + strip
+                part = jnp.dot(
+                    weights.astype(jnp.bfloat16), values[start:start + size, :],
+                    preferred_element_type=jnp.float32,
+                )
+                mixed = part if mixed is None else mixed + part
+            out = (mixed / jnp.sum(total, axis=-1, keepdims=True)).astype(jnp.bfloat16)
+            cols = pl.ds(pl.multiple_of(g * HEAD_SIZE, HEAD_SIZE), HEAD_SIZE)
             share = block // head_count
-            for u in range(pair):
-                out = (states[u][2] / states[u][1]).astype(jnp.bfloat16)
-                cols = pl.ds(pl.multiple_of((i * pair + u) * HEAD_SIZE, HEAD_SIZE), HEAD_SIZE)
-                for h in range(head_count):
-                    stage_a[j][h, :, cols] = out[h * share:(h + 1) * share, :]
+            for h in range(head_count):
+                stage_a[j][h, :, cols] = out[h * share:(h + 1) * share, :]
+
+        def hooks(i):
+            @pl.when(i == 0)
+            def _():
+                send_out(j, steps)
+
+            @pl.when(i > 0)
+            def _():
+                send_out(j, i - 1)
+
+            third = -(-len(offsets) // 3)
+            everything = list(range(len(offsets)))
+            plan = [[] for _ in range(steps)]
+            if j == 0:
+                plan[0] += [(1, k) for k in everything] + [(2, None)]
+                plan[1] += [(2, k) for k in everything[:third]]
+                plan[2] += [(2, k) for k in everything[third:2 * third]]
+            elif j == 1:
+                plan[0] += [(2, k) for k in everything[2 * third:]] + [(3, None)]
+            if j > 0:
+                plan[1] += [(j + 2, k) for k in everything[:third]]
+                plan[2] += [(j + 2, k) for k in everything[third:]] + [(j + 3, None)]
+            for at, actions in enumerate(plan):
+                @pl.when(i == at)
+                def _(at=at, actions=actions):
+                    for target, k in actions:
+                        if k is None:
+                            x_own(target)
+                        else:
+                            forward_z(target, k)
+                    if at >= steps - 2:
+                        forward_x(j + 1, at - (steps - 2))
+
+        def step(i, carry):
+            first_pass(2 * i + 1, 1)
+            second_pass(2 * i, 0)
+            first_pass(jnp.minimum(2 * i + 2, group - 1), 0)
+            second_pass(2 * i + 1, 1)
+            hooks(i)
             return carry
 
+        first_pass(0, 0)
         lax.fori_loop(0, steps, step, 0)
-        forward_x(j + 1)
-
-        cols = pl.ds(pl.multiple_of((head * heads_kv + j) * width, width), width)
-        for n, (staged, result) in enumerate(((stage_a[j], aout_ref), (stage_p[j], pout_ref))):
-            for k in range(1, head_count):
-                target = (head + k) % head_count
-                copy = pltpu.make_async_remote_copy(
-                    src_ref=staged.at[target], dst_ref=result.at[:, cols],
-                    send_sem=out_send.at[j, n, k], recv_sem=out_recv.at[j, n, head],
-                    device_id=(me, target), device_id_type=MESH,
-                )
-                copy.start()
-                sends.append((j, copy))
-            local = pltpu.make_async_copy(staged.at[head], result.at[:, cols], out_local.at[j, n])
-            local.start()
-            out_copies.append(local)
-
-    for local in out_copies:
-        local.wait()
+
+        send_out(j, steps - 1)
+
+    def out_parts():
+        for j in range(heads_kv):
+            for i in range(steps + 1):
+                yield j, i
+
+    for j, i in out_parts():
+        out_copy(j, i).wait()
+    for j, i in out_parts():
+        for k in range(1, head_count):
+            out_remote(j, i, k, (head + k) % head_count).wait_recv()
     for j in range(heads_kv):
-        for k in range(1, head_count):
-            other = (head + k) % head_count
-            cols = pl.ds(pl.multiple_of((other * heads_kv + j) * width, width), width)
-            for n, (staged, result) in enumerate(((stage_a[j], aout_ref), (stage_p[j], pout_ref))):
-                pltpu.make_async_remote_copy(
-                    src_ref=staged.at[other], dst_ref=result.at[:, cols],
-                    send_sem=out_send.at[j, n, k], recv_sem=out_recv.at[j, n, other],
-                    device_id=(me, other), device_id_type=MESH,
-                ).wait_recv()
-    for j in range(heads_kv):
-        for k in offsets:
-            wait_sent(pieces[j].at[me], z_sem.at[j, k], c_peer, head)
+        if relayed:
+            for k in range(2):
+                wait_sent(pieces[j].at[me], z_sem.at[j, k], c_peer, head)
+
+            @pl.when(inner == 1)
+            def _(j=j):
+                for k in range(2):
+                    wait_sent(pieces[j].at[me], z_sem.at[j, 2 + k], c_peer, head)
+        else:
+            for k in offsets:
+                wait_sent(pieces[j].at[me], z_sem.at[j, k], c_peer, head)
         for k in range(z_count):
             wait_sent(pieces[j].at[me], x_sem.at[j, k], c_peer, head)
             for n in range(2):
                 wait_sent(pieces[j].at[me], c_sem.at[j, n, k], c_peer, head)
-        for n, staged in enumerate((stage_a[j], stage_p[j])):
-            for k in range(1, head_count):
-                wait_sent(staged.at[0], out_send.at[j, n, k], c_peer, head)
+    for j, i in out_parts():
+        for k in range(1, head_count):
+            out_remote(j, i, k, (head + k) % head_count).wait_send()
 
 
 def wait_sent(ref, sem, peer, head):
@@ -307,7 +404,6 @@
     dma = pltpu.SemaphoreType.DMA
     any_space = pl.BlockSpec(memory_space=pl.ANY)
     smem = pl.BlockSpec(memory_space=pltpu.SMEM)
-    vmem = pl.BlockSpec(memory_space=pltpu.VMEM)
     return pl.pallas_call(
         functools.partial(kernel, seq_count, head_count, heads_kv, group, most, 512),
         out_shape=(
@@ -315,7 +411,7 @@
             jax.ShapeDtypeStruct((block // head_count, rq.shape[1] * head_count), jnp.bfloat16),
         ),
         in_specs=[smem] * 2 + [any_space] * 6,
-        out_specs=(vmem, vmem),
+        out_specs=(any_space, any_space),
         scratch_shapes=(
             [pltpu.VMEM((seq_count, 2 * (block + prompt_rows), HEAD_SIZE), jnp.bfloat16)] * heads_kv
             + [pltpu.VMEM((head_count, block // head_count, width), jnp.bfloat16)] * heads_kv
@@ -328,13 +424,16 @@
                 dma((heads_kv, 4)),
                 dma((2,)),
                 dma((heads_kv, seq_count)),
-                dma((heads_kv, z_count)),
+                dma((heads_kv, max(z_count, 4))),
                 dma((heads_kv, z_count)),
                 dma((heads_kv, 2, z_count)),
-                dma((heads_kv, 2, head_count)),
-                dma((heads_kv, 2, head_count)),
-                dma((heads_kv, 2)),
+                dma((heads_kv, group // 2 + 1, head_count)),
+                dma((heads_kv, group // 2 + 1, head_count)),
+                dma((heads_kv, group // 2 + 1)),
+                pltpu.VMEM((block, most * block), jnp.float32),
             ]
+            + [pltpu.VMEM((block, total), jnp.float32)] * 2
+            + [pltpu.VMEM((block, HEAD_SIZE), jnp.float32)] * 2
         ),
         compiler_params=pltpu.CompilerParams(
             collective_id=0, has_side_effects=True, vmem_limit_bytes=60 * 1024 * 1024

time: 95.3 us -> 78.3 us (0.82)
  Pallas kernels: 90.1 us -> 73.2 us
    pallas_call x1, Pallas kernels: 90.1 us -> 73.2 us  [on_device(): pl.pallas_call(functools.partial(kernel, seq_count, head_count, heads_kv,...]
where the time goes in v2:
time: 78.3 us; the launch traced here: 78.1 us
  Pallas kernels  73.2 us (93%)
  local copies, waits for them, and re-layouts  4.32 us (6%)
    pallas_call x1, Pallas kernels, on_device(): pl.pallas_call(functools.partial(kernel, seq_count, head_count, heads_kv,...  73.2 us
    unnamed x2, local copies, waits for them, and re-layouts  4.32 us

profile of v2, /device:TPU:0, one launch (start us, length us, event | category | flops | bytes accessed | tf_op | source)
XLA Modules:
  0.0 78.1 jit_solution(6943550542023833948)
XLA Ops:
  0.6 73.2 %shard_map.95 = (bf16[16,8192]{1,0:T(8,128)(2,1)}, bf16[96,8192]{1,0:T(8,128)(2,1)}) custom-call(s32[4]{0:T(128)} %lengths_ref.1, s32[16]{0:T(128)} %table_ref.1, bf16[32,4096]{1,0:T(8,128)(2,1)} %pq_hbm.1, bf16[32,512]{1,0:T(8,128)(2,1)} %pk_hbm.1, bf16[32,512]{1,0:T(8,128)(2,1)} %pv_hbm.1, bf16[192,4096]{1,0:T(8,128)(2,1)} %rq_hbm.1, ...), custom_call_target="tpu_custom_call" | custom-call | tf_op jit(solution)/shard_map/pallas_call | solution.py:407
  73.8 1.7 %copy.12 = bf16[16,8192]{1,0:T(8,128)(2,1)} copy(bf16[16,8192]{1,0:T(8,128)(2,1)} %get-tuple-element.4) | data formatting | bytes 524288
  75.5 2.7 %copy.13 = bf16[96,8192]{1,0:T(8,128)(2,1)} copy(bf16[96,8192]{1,0:T(8,128)(2,1)} %get-tuple-element.5) | data formatting | bytes 3145728

commit v3 on v2

--- a/solution.py
+++ b/solution.py
@@ -201,6 +201,7 @@
     for k in range(len(offsets)):
         forward_z(0, k)
     x_own(1)
+    x_own(2)
     forward_x(0, 0)
     forward_x(0, 1)
     for copy in q_copies:
@@ -322,11 +323,11 @@
             everything = list(range(len(offsets)))
             plan = [[] for _ in range(steps)]
             if j == 0:
-                plan[0] += [(1, k) for k in everything] + [(2, None)]
+                plan[0] += [(1, k) for k in everything] + [(3, None)]
                 plan[1] += [(2, k) for k in everything[:third]]
                 plan[2] += [(2, k) for k in everything[third:2 * third]]
             elif j == 1:
-                plan[0] += [(2, k) for k in everything[2 * third:]] + [(3, None)]
+                plan[0] += [(2, k) for k in everything[2 * third:]]
             if j > 0:
                 plan[1] += [(j + 2, k) for k in everything[:third]]
                 plan[2] += [(j + 2, k) for k in everything[third:]] + [(j + 3, None)]

time: 78.3 us -> 76.6 us (0.978)
  Pallas kernels: 73.2 us -> 71.4 us
    pallas_call x1, Pallas kernels: 73.2 us -> 71.4 us  [on_device(): pl.pallas_call(functools.partial(kernel, seq_count, head_count, heads_kv,...]
where the time goes in v3:
time: 76.6 us; the launch traced here: 76.4 us
  Pallas kernels  71.4 us (93%)
  local copies, waits for them, and re-layouts  4.32 us (6%)
    pallas_call x1, Pallas kernels, on_device(): pl.pallas_call(functools.partial(kernel, seq_count, head_count, heads_kv,...  71.4 us
    unnamed x2, local copies, waits for them, and re-layouts  4.32 us

profile of v3, /device:TPU:0, one launch (start us, length us, event | category | flops | bytes accessed | tf_op | source)
XLA Modules:
  0.0 76.4 jit_solution(4549758000679389708)
XLA Ops:
  0.6 71.4 %shard_map.95 = (bf16[16,8192]{1,0:T(8,128)(2,1)}, bf16[96,8192]{1,0:T(8,128)(2,1)}) custom-call(s32[4]{0:T(128)} %lengths_ref.1, s32[16]{0:T(128)} %table_ref.1, bf16[32,4096]{1,0:T(8,128)(2,1)} %pq_hbm.1, bf16[32,512]{1,0:T(8,128)(2,1)} %pk_hbm.1, bf16[32,512]{1,0:T(8,128)(2,1)} %pv_hbm.1, bf16[192,4096]{1,0:T(8,128)(2,1)} %rq_hbm.1, ...), custom_call_target="tpu_custom_call" | custom-call | tf_op jit(solution)/shard_map/pallas_call | solution.py:408
  72.1 1.7 %copy.12 = bf16[16,8192]{1,0:T(8,128)(2,1)} copy(bf16[16,8192]{1,0:T(8,128)(2,1)} %get-tuple-element.4) | data formatting | bytes 524288
  73.7 2.7 %copy.13 = bf16[96,8192]{1,0:T(8,128)(2,1)} copy(bf16[96,8192]{1,0:T(8,128)(2,1)} %get-tuple-element.5) | data formatting | bytes 3145728
